TPU v7x, 256 devices: a whole 4x4x8 slice. The times are simulated.
256 devices in a mesh: snap: 8 (over z), vert: 32 (over x, y, core).
Axes of the slice: x: 4, y: 4, z: 8, core: 2. Of those that a mesh axis runs over, the one named last changes fastest.
Arguments:
- features: bfloat16 [16, 65536, 256], P('snap', 'vert'), may hold values from -6 to 6
- tile_rows: int32 [16, 2048], P('snap', 'vert'), may hold values from 0 to 15
- tile_cols: int32 [16, 2048], P('snap', 'vert'), may hold values from 0 to 21
- tile_vals: bfloat16 [16, 2048, 128, 128], P('snap', 'vert'), may hold values from -0.25 to 0.25
- send_lists: int32 [32, 6], replicated, may hold values from 0 to 15
- conv1_weight: bfloat16 [256, 256], replicated, may hold values from -0.375 to 0.375
- conv2_weight: bfloat16 [256, 256], replicated, may hold values from -0.375 to 0.375
- lstm_weight: bfloat16 [2, 512, 1024], replicated, may hold values from -0.25 to 0.25
- lstm_bias: float32 [2, 1024], replicated, may hold values from -4 to 4
Outputs:
- mixed: bfloat16 [16, 65536, 256], P('snap', 'vert')
All inputs are finite; a program needn't handle non-finite values.
Results may differ from a plain program's by a relative error of at most 0.007.
Values may be sent and summed in bfloat16 or wider, within the bound.
A program may use at most 128 MiB of HBM per device.

v0:
```python
import jax
import jax.numpy as jnp
from jax import lax
from jax.sharding import PartitionSpec as P

BS = 128


def with_halo(block, sides, width):
    for axis, dim in sides:
        count = lax.axis_size(axis)
        forward = [(i, i + 1) for i in range(count - 1)]
        forward.append((count - 1, 0))
        backward = [(target, source) for source, target in forward]
        low = lax.ppermute(
            lax.slice_in_dim(block, block.shape[dim] - width, None, axis=dim), axis, forward
        )
        high = lax.ppermute(lax.slice_in_dim(block, 0, width, axis=dim), axis, backward)
        block = jnp.concatenate([low, block, high], axis=dim)
    return block


def rims(packed, width):
    return with_halo(packed, (("vert", 1),), width)


def extend(field, send_lists, tile_cols):
    snapshots, vertices, width = field.shape
    blocks = vertices // BS
    bound = send_lists.shape[1] // 2
    device = lax.axis_index("vert")
    own_list = lax.dynamic_index_in_dim(send_lists, device, 0, keepdims=False)
    packed = jnp.take(field.reshape(snapshots, blocks, BS, width), own_list, axis=1).reshape(
        snapshots, 2 * bound * BS, width
    )
    bordered = rims(packed, bound * BS)
    extended = jnp.concatenate(
        [bordered[:, : bound * BS], field, bordered[:, bordered.shape[1] - bound * BS :]], axis=1
    )
    return (extended.reshape(snapshots, -1, BS, width), tile_cols)


def convolve(field, tile_rows, tile_cols, tile_vals, send_lists):
    snapshots, vertices, width = field.shape
    blocks = vertices // BS
    extended, position = extend(field, send_lists, tile_cols)
    picked = jax.vmap(lambda slab, where_at: jnp.take(slab, where_at, axis=0))(extended, position)
    product = jnp.einsum("skij,skjf->skif", tile_vals, picked, preferred_element_type=jnp.float32)
    onehot = (tile_rows[..., None] == jnp.arange(blocks, dtype=jnp.int32)).astype(jnp.float32)
    summed = jnp.einsum("skb,skif->sbif", onehot, product, preferred_element_type=jnp.float32)
    return summed.reshape(snapshots, vertices, width)


def project(field, weight):
    snapshots, vertices, width = field.shape
    result = jnp.dot(
        field.reshape(snapshots * vertices, width), weight, preferred_element_type=jnp.float32
    )
    return result.astype(jnp.bfloat16).reshape(snapshots, vertices, width)


def cell_step(inputs, hidden, memory, weight, bias):
    gates = (
        jnp.dot(
            jnp.concatenate([inputs, hidden], axis=-1), weight, preferred_element_type=jnp.float32
        )
        + bias
    )
    in_gate, forget, candidate, out_gate = jnp.split(gates, 4, axis=-1)
    memory = jax.nn.sigmoid(forget) * memory + jax.nn.sigmoid(in_gate) * jnp.tanh(candidate)
    hidden = (jax.nn.sigmoid(out_gate) * jnp.tanh(memory)).astype(jnp.bfloat16)
    return (hidden, memory)


def shards(
    features,
    tile_rows,
    tile_cols,
    tile_vals,
    send_lists,
    conv1_weight,
    conv2_weight,
    lstm_weight,
    lstm_bias,
):
    snapshots, vertices, width = features.shape
    projected = project(features, conv1_weight)
    convolved = jnp.maximum(
        convolve(projected, tile_rows, tile_cols, tile_vals, send_lists), 0.0
    ).astype(jnp.bfloat16)
    groups = lax.axis_size("snap")
    grouped = convolved.reshape(snapshots, groups, vertices // groups, width)
    sequence = lax.all_to_all(grouped, "snap", split_axis=1, concat_axis=0, tiled=True)[:, 0]
    count = sequence.shape[1]
    zero_h = jnp.zeros((count, width), jnp.bfloat16)
    zero_c = jnp.zeros((count, width), jnp.float32)

    def advance(carry, inputs):
        first_h, first_c, second_h, second_c = carry
        first_h, first_c = cell_step(inputs, first_h, first_c, lstm_weight[0], lstm_bias[0])
        second_h, second_c = cell_step(first_h, second_h, second_c, lstm_weight[1], lstm_bias[1])
        return ((first_h, first_c, second_h, second_c), second_h)

    carry, outputs = lax.scan(advance, (zero_h, zero_c, zero_h, zero_c), sequence)
    recurrent = outputs[:, None]
    restored = lax.all_to_all(recurrent, "snap", split_axis=0, concat_axis=1, tiled=True).reshape(
        snapshots, vertices, width
    )
    second = project(restored, conv2_weight)
    return convolve(second, tile_rows, tile_cols, tile_vals, send_lists).astype(jnp.bfloat16)


def solution(mesh):
    placed = (
        P("snap", "vert", None),
        P("snap", "vert"),
        P("snap", "vert"),
        P("snap", "vert", None, None),
        P(),
        P(),
        P(),
        P(),
        P(),
    )
    return jax.shard_map(
        shards, mesh=mesh, in_specs=placed, out_specs=P("snap", "vert", None), check_vma=False
    )
```

profile of v0, /device:TPU:64, one launch (start us, length us, event | category | flops | bytes accessed | tf_op | source)
XLA Modules:
  0.0 302.1 jit_solution(4708403883143465019)
XLA Ops:
  0.0 1.0 dynamic-slice_reduce_fusion
  1.1 0.6 copy-done
  1.6 2.9 convolution_convert_fusion.1
  4.5 2.2 gather_fusion
  7.1 5.1 %collective-permute-start.1 = (bf16[2,384,256]{2,1,0:T(8,128)(2,1)S(1)}, bf16[2,384,256]{2,1,0:T(8,128)(2,1)S(1)}, u32[]{:S(2)}, u32[]{:S(2)}) collective-permute-start(bf16[2,384,256]{2,1,0:T(8,128)(2,1)S(1)} %get-tuple-element.115), channel_id=1, source_target_pairs={{1,0},{2,1},{3,2},{4,3},{5,4},{6,5},{7,6},{8,7},{9,8},{10,9},{11,1... | collective-permute-start | bytes 1179656 | tf_op jit(solution)/shard_map/ppermute | solution.py:18
  12.3 5.4 %collective-permute-done = bf16[2,384,256]{2,1,0:T(8,128)(2,1)S(1)} collective-permute-done((bf16[2,384,256]{2,1,0:T(8,128)(2,1)S(1)}, bf16[2,384,256]{2,1,0:T(8,128)(2,1)S(1)}, u32[]{:S(2)}, u32[]{:S(2)}) %collective-permute-start) | collective-permute-done | bytes 393248 | tf_op jit(solution)/shard_map/ppermute | solution.py:15
  17.6 0.7 copy-done.3
  18.4 1.9 pad_maximum_fusion
  20.3 7.2 %gather_fusion.1 = bf16[128,128,256]{2,1,0:T(8,128)(2,1)} fusion(bf16[2,22,128,256]{3,2,1,0:T(8,128)(2,1)S(1)} %bitcast.76, s32[128]{0:T(128)S(1)} %reshape.92), kind=kCustom, calls=%fused_computation.1.clone | custom fusion | bytes 16778240 | tf_op jit(solution)/shard_map/vmap(jit(_take))/gather | solution.py:47
  27.5 12.0 %copy.35 = bf16[2,64,128,256]{2,3,1,0:T(8,128)(2,1)} copy(bf16[2,64,128,256]{3,2,1,0:T(8,128)(2,1)} %bitcast.78) | data formatting | bytes 16777216 | tf_op jit(solution)/shard_map/vmap(jit(_take))/gather | solution.py:47
  39.5 11.6 %fusion.46 = bf16[2,64,128,256]{2,3,1,0:T(8,128)(2,1)} fusion(bf16[2,64,128,128]{3,2,1,0:T(8,128)(2,1)} %param.18, bf16[2,64,128,256]{2,3,1,0:T(8,128)(2,1)} %copy.35, pred[2,64]{1,0:T(4,128)(4,1)S(1)} %compare_and_fusion), kind=kOutput, calls=%fused_computation.64 | convolution fusion | flops 1077936128 | bytes 20971648 | tf_op jit(solution)/shard_map/skij,skjf->skif/dot_general | solution.py:48
  51.1 12.3 %copy.36 = bf16[2,64,128,256]{3,1,2,0:T(8,128)(2,1)} copy(bf16[2,64,128,256]{2,3,1,0:T(8,128)(2,1)} %fusion.46) | data formatting | bytes 16777216 | tf_op jit(solution)/shard_map/skij,skjf->skif/dot_general | solution.py:48
  63.4 4.6 %maximum_convert_fusion = bf16[2,16,128,256]{3,1,2,0:T(8,128)(2,1)S(1)} fusion(bf16[2,64,128,256]{3,1,2,0:T(8,128)(2,1)} %copy.36, s32[2,64]{1,0:T(2,128)S(1)} %copy-done.6), kind=kOutput, calls=%fused_computation.70 | convolution fusion | flops 137365504 | bytes 10486272 | tf_op jit(solution)/shard_map/skb,skif->sbif/dot_general | solution.py:50
  68.0 0.7 copy.37
  68.8 1.5 copy.38
  70.3 8.1 %all-to-all-start = ((bf16[2,8,256,256]{3,2,0,1:T(8,128)(2,1)}), bf16[2,8,256,256]{3,2,0,1:T(8,128)(2,1)S(1)}, u32[]{:S(2)}, u32[]{:S(2)}) async-start(bf16[2,8,256,256]{3,2,0,1:T(8,128)(2,1)} %copy.38), calls=%async_computation | async-start | bytes 4194304 | tf_op jit(solution)/shard_map/all_to_all | solution.py:93
  78.4 47.5 %all-to-all-done = bf16[2,8,256,256]{3,2,0,1:T(8,128)(2,1)S(1)} async-done(((bf16[2,8,256,256]{3,2,0,1:T(8,128)(2,1)}), bf16[2,8,256,256]{3,2,0,1:T(8,128)(2,1)S(1)}, u32[]{:S(2)}, u32[]{:S(2)}) %all-to-all-start) | async-done | bytes 2097184 | tf_op jit(solution)/shard_map/all_to_all | solution.py:93
  125.9 57.3 %while.19 = (s32[]{:T(128)}, bf16[256,256]{1,0:T(8,128)(2,1)S(1)}, f32[256,256]{1,0:T(8,128)S(1)}, bf16[256,256]{1,0:T(8,128)(2,1)S(1)}, f32[256,256]{1,0:T(8,12...) while((s32[]{:T(128)}, bf16[256,256]{1,0:T(8,128)(2,1)S(1)}, ...), condition=%wide.region_1.4_spmd.clone, body=%wide.region_0.0_spmd.clone.sunk | while | flops 540540928 | bytes 17457816 | solution.py:104
  126.0 1.8 convolution_add_fusion.4
  128.6 0.9 bitcast_dynamic-update-slice_fusion.2
  129.6 1.8 convolution_add_fusion.4
  132.1 0.9 bitcast_dynamic-update-slice_fusion.2
  133.2 1.8 convolution_add_fusion.4
  135.7 0.9 bitcast_dynamic-update-slice_fusion.2
  136.7 1.8 convolution_add_fusion.4
  139.3 0.9 bitcast_dynamic-update-slice_fusion.2
  140.3 1.8 convolution_add_fusion.4
  142.9 0.9 bitcast_dynamic-update-slice_fusion.2
  143.9 1.8 convolution_add_fusion.4
  146.5 0.9 bitcast_dynamic-update-slice_fusion.2
  147.5 1.8 convolution_add_fusion.4
  150.1 0.9 bitcast_dynamic-update-slice_fusion.2
  151.1 1.8 convolution_add_fusion.4
  153.6 0.9 bitcast_dynamic-update-slice_fusion.2
  154.7 1.8 convolution_add_fusion.4
  156.8 0.4 convolution_add_fusion.5
  157.2 0.9 bitcast_dynamic-update-slice_fusion.2
  158.2 1.8 convolution_add_fusion.4
  160.8 0.9 bitcast_dynamic-update-slice_fusion.2
  161.8 1.8 convolution_add_fusion.4
  163.9 0.4 convolution_add_fusion.5
  164.4 0.9 bitcast_dynamic-update-slice_fusion.2
  165.4 1.8 convolution_add_fusion.4
  168.0 0.9 bitcast_dynamic-update-slice_fusion.2
  169.0 1.8 convolution_add_fusion.4
  171.6 0.9 bitcast_dynamic-update-slice_fusion.2
  172.6 1.8 convolution_add_fusion.4
  175.1 0.9 bitcast_dynamic-update-slice_fusion.2
  176.2 1.8 convolution_add_fusion.4
  178.7 0.9 bitcast_dynamic-update-slice_fusion.2
  179.7 1.8 convolution_add_fusion.4
  182.3 0.9 bitcast_dynamic-update-slice_fusion.2
  183.3 54.7 %all_to_all.30 = bf16[16,1,256,256]{3,2,1,0:T(8,128)(2,1)S(1)} all-to-all(bf16[16,1,256,256]{3,2,1,0:T(8,128)(2,1)} %bitcast.89), channel_id=1, replica_groups=mesh['snap'=8,'vert'=32] {'snap'}, dimensions={0} | all-to-all | bytes 4194304 | tf_op jit(solution)/shard_map/all_to_all | solution.py:106
  238.2 0.7 convolution_convert_fusion
  238.9 0.6 gather_fusion.2
  239.9 5.1 %collective-permute-start.3 = (bf16[2,384,256]{2,1,0:T(8,128)(2,1)S(1)}, bf16[2,384,256]{2,1,0:T(8,128)(2,1)S(1)}, u32[]{:S(2)}, u32[]{:S(2)}) collective-permute-start(bf16[2,384,256]{2,1,0:T(8,128)(2,1)S(1)} %get-tuple-element.113), channel_id=1, source_target_pairs={{1,0},{2,1},{3,2},{4,3},{5,4},{6,5},{7,6},{8,7},{9,8},{10,9},{11,1... | collective-permute-start | bytes 1179656 | tf_op jit(solution)/shard_map/ppermute | solution.py:18
  244.9 5.5 %collective-permute-done.2 = bf16[2,384,256]{2,1,0:T(8,128)(2,1)S(1)} collective-permute-done((bf16[2,384,256]{2,1,0:T(8,128)(2,1)S(1)}, bf16[2,384,256]{2,1,0:T(8,128)(2,1)S(1)}, u32[]{:S(2)}, u32[]{:S(2)}) %collective-permute-start.2) | collective-permute-done | bytes 393248 | tf_op jit(solution)/shard_map/ppermute | solution.py:15
  250.4 1.8 pad_maximum_fusion.1
  252.2 7.2 %gather_fusion.3 = bf16[128,128,256]{2,1,0:T(8,128)(2,1)} fusion(bf16[2,22,128,256]{3,2,1,0:T(8,128)(2,1)S(1)} %bitcast.75, s32[128]{0:T(128)S(1)} %reshape.92), kind=kCustom, calls=%fused_computation.3.clone | custom fusion | bytes 16778240 | tf_op jit(solution)/shard_map/vmap(jit(_take))/gather | solution.py:47
  259.4 12.0 %copy.41 = bf16[2,64,128,256]{2,3,1,0:T(8,128)(2,1)} copy(bf16[2,64,128,256]{3,2,1,0:T(8,128)(2,1)} %bitcast.77) | data formatting | bytes 16777216 | tf_op jit(solution)/shard_map/vmap(jit(_take))/gather | solution.py:47
  271.4 11.6 %fusion.49 = bf16[2,64,128,256]{2,3,1,0:T(8,128)(2,1)} fusion(bf16[2,64,128,128]{3,2,1,0:T(8,128)(2,1)} %param.18, bf16[2,64,128,256]{2,3,1,0:T(8,128)(2,1)} %copy.41, pred[2,64]{1,0:T(4,128)(4,1)S(1)} %compare_and_fusion), kind=kOutput, calls=%fused_computation.65 | convolution fusion | flops 1077936128 | bytes 20971648 | tf_op jit(solution)/shard_map/skij,skjf->skif/dot_general | solution.py:48
  283.0 12.3 %copy.42 = bf16[2,64,128,256]{3,1,2,0:T(8,128)(2,1)} copy(bf16[2,64,128,256]{2,3,1,0:T(8,128)(2,1)} %fusion.49) | data formatting | bytes 16777216 | tf_op jit(solution)/shard_map/skij,skjf->skif/dot_general | solution.py:48
  295.3 4.7 %convolution_convert_fusion.2 = bf16[2,16,128,256]{3,1,2,0:T(8,128)(2,1)S(1)} fusion(bf16[2,64,128,256]{3,1,2,0:T(8,128)(2,1)} %copy.42, s32[2,64]{1,0:T(2,128)S(1)} %copy-done.6), kind=kOutput, calls=%fused_computation.73 | convolution fusion | flops 134219776 | bytes 10486272 | tf_op jit(solution)/shard_map/skb,skif->sbif/dot_general | solution.py:50
  300.0 2.1 copy.43
  (146 shorter events, 12.6 us)
Async XLA Ops:
  0.0 1.6 copy-start
  4.5 7.6 %copy-start.7 = (s32[2,64]{1,0:T(2,128)S(1)}, s32[2,64]{1,0:T(2,128)}, u32[]{:S(2)}) copy-start(s32[2,64]{1,0:T(2,128)} %param.17) | copy-start | bytes 1540
  7.0 10.6 %collective-permute-start = (bf16[2,384,256]{2,1,0:T(8,128)(2,1)S(1)}, bf16[2,384,256]{2,1,0:T(8,128)(2,1)S(1)}, u32[]{:S(2)}, u32[]{:S(2)}) collective-permute-start(bf16[2,384,256]{2,1,0:T(8,128)(2,1)S(1)} %get-tuple-element.114), channel_id=1, source_target_pairs={{0,1},{1,2},{2,3},{3,4},{4,5},{5,6},{6,7},{7,8},{8,9},{9,10},{10,1... | collective-permute-start | bytes 1179656 | tf_op jit(solution)/shard_map/ppermute | solution.py:15
  7.1 10.5 %collective-permute-start.1 = (bf16[2,384,256]{2,1,0:T(8,128)(2,1)S(1)}, bf16[2,384,256]{2,1,0:T(8,128)(2,1)S(1)}, u32[]{:S(2)}, u32[]{:S(2)}) collective-permute-start(bf16[2,384,256]{2,1,0:T(8,128)(2,1)S(1)} %get-tuple-element.115), channel_id=1, source_target_pairs={{1,0},{2,1},{3,2},{4,3},{5,4},{6,5},{7,6},{8,7},{9,8},{10,9},{11,1... | collective-permute-start | bytes 1179656 | tf_op jit(solution)/shard_map/ppermute | solution.py:18
  17.6 0.7 copy-start.3
  51.1 12.3 %copy-start.6 = (s32[2,64]{1,0:T(2,128)S(1)}, s32[2,64]{1,0:T(2,128)}, u32[]{:S(2)}) copy-start(s32[2,64]{1,0:T(2,128)} %param.16) | copy-start | bytes 1540
  68.8 57.2 %copy-start.4 = (f32[2,1024]{1,0:T(2,128)S(1)}, f32[2,1024]{1,0:T(2,128)}, u32[]{:S(2)}) copy-start(f32[2,1024]{1,0:T(2,128)} %param.23) | copy-start | bytes 24580
  70.3 55.7 %all-to-all-start = ((bf16[2,8,256,256]{3,2,0,1:T(8,128)(2,1)}), bf16[2,8,256,256]{3,2,0,1:T(8,128)(2,1)S(1)}, u32[]{:S(2)}, u32[]{:S(2)}) async-start(bf16[2,8,256,256]{3,2,0,1:T(8,128)(2,1)} %copy.38), calls=%async_computation | async-start | bytes 4194304 | tf_op jit(solution)/shard_map/all_to_all | solution.py:93
  125.9 2.2 copy-start.8
  129.5 2.2 copy-start.8
  133.1 2.2 copy-start.8
  136.7 2.2 copy-start.8
  140.3 2.2 copy-start.8
  143.8 2.2 copy-start.8
  147.4 2.2 copy-start.8
  151.0 2.2 copy-start.8
  154.6 2.2 copy-start.8
  158.2 2.2 copy-start.8
  161.8 2.2 copy-start.8
  165.3 2.2 copy-start.8
  168.9 2.2 copy-start.8
  172.5 2.2 copy-start.8
  176.1 2.2 copy-start.8
  179.7 2.2 copy-start.8
  183.3 54.9 %copy-start.5 = (bf16[256,256]{1,0:T(8,128)(2,1)S(1)}, bf16[256,256]{1,0:T(8,128)(2,1)}, u32[]{:S(2)}) copy-start(bf16[256,256]{1,0:T(8,128)(2,1)} %param.21) | copy-start | bytes 393220
  238.9 11.5 %copy-start.2 = (bf16[4096,256]{1,0:T(8,128)(2,1)}, bf16[4096,256]{1,0:T(8,128)(2,1)S(1)}, u32[]{:S(2)}) copy-start(bf16[4096,256]{1,0:T(8,128)(2,1)S(1)} %convolution_convert_fusion) | copy-start | bytes 6291460
  239.8 10.6 %collective-permute-start.2 = (bf16[2,384,256]{2,1,0:T(8,128)(2,1)S(1)}, bf16[2,384,256]{2,1,0:T(8,128)(2,1)S(1)}, u32[]{:S(2)}, u32[]{:S(2)}) collective-permute-start(bf16[2,384,256]{2,1,0:T(8,128)(2,1)S(1)} %get-tuple-element.112), channel_id=1, source_target_pairs={{0,1},{1,2},{2,3},{3,4},{4,5},{5,6},{6,7},{7,8},{8,9},{9,10},{10,1... | collective-permute-start | bytes 1179656 | tf_op jit(solution)/shard_map/ppermute | solution.py:15
  239.9 10.5 %collective-permute-start.3 = (bf16[2,384,256]{2,1,0:T(8,128)(2,1)S(1)}, bf16[2,384,256]{2,1,0:T(8,128)(2,1)S(1)}, u32[]{:S(2)}, u32[]{:S(2)}) collective-permute-start(bf16[2,384,256]{2,1,0:T(8,128)(2,1)S(1)} %get-tuple-element.113), channel_id=1, source_target_pairs={{1,0},{2,1},{3,2},{4,3},{5,4},{6,5},{7,6},{8,7},{9,8},{10,9},{11,1... | collective-permute-start | bytes 1179656 | tf_op jit(solution)/shard_map/ppermute | solution.py:18
  295.3 6.8 %copy-start.1 = (bf16[2,2048,256]{2,1,0:T(8,128)(2,1)S(1)}, bf16[2,2048,256]{2,1,0:T(8,128)(2,1)}, u32[]{:S(2)}) copy-start(bf16[2,2048,256]{2,1,0:T(8,128)(2,1)} %param.15) | copy-start | bytes 6291460
where the time goes:
time: 307 us; the launch traced here: 302 us
  local copies, waits for them, and re-layouts  73.4 us (24%)
  matrix products  72.1 us (23%)
  waiting for transfers between devices  58.4 us (19%)
  blocking collectives  54.7 us (18%)
  other arithmetic  24.2 us (8%)
  starting transfers between devices  18.4 us (6%)
    all_to_all x1, blocking collectives, shards(): lax.all_to_all(recurrent, 'snap', split_axis=0, concat_axis=1, tiled=True)  54.7 us
    all_to_all x1, waiting for transfers between devices, shards(): lax.all_to_all(grouped, 'snap', split_axis=1, concat_axis=0, tiled=True)  47.5 us
    gather x5, local copies, waits for them, and re-layouts, convolve(): jnp.take(slab, where_at, axis=0)  38.5 us
    dot_general x32, matrix products, cell_step(): jnp.dot(jnp.concatenate([inputs, hidden], axis=-1), weight, preferred_ele...  35.9 us
    dot_general x2, local copies, waits for them, and re-layouts, convolve(): jnp.einsum('skij,skjf->skif', tile_vals, picked, preferred_element_type=j...  24.5 us
    dot_general x2, matrix products, convolve(): jnp.einsum('skij,skjf->skif', tile_vals, picked, preferred_element_type=j...  23.2 us
    dynamic_update_slice x16, other arithmetic, shards(): lax.scan(advance, (zero_h, zero_c, zero_h, zero_c), sequence)  15.2 us
    ppermute x2, waiting for transfers between devices, with_halo(): lax.ppermute(lax.slice_in_dim(block, block.shape[dim] - width, None, axis...  10.8 us
  transfers between devices with their start and end apart: 5, of which 3 were waited for; matrix products, arithmetic and copies ran while one was open for 0% of the time, Pallas kernels for 0%

commit v1 on v0

v1 whole, which is shorter than its diff:
```python
import functools

import jax
import jax.numpy as jnp
from jax import lax
from jax.experimental import pallas as pl
from jax.experimental.pallas import tpu as pltpu
from jax.sharding import PartitionSpec as P

BS = 128
MESH = pl.DeviceIdType.MESH
UNROLL = 8


def conv_kernel(project, relu, rows, cols, own, halo, vals, *rest):
    if project:
        weight, out, extended, acc = rest
    else:
        out, extended, acc = rest
    snap = pl.program_id(0)
    blocks = own.shape[1]
    bound = halo.shape[2]

    def put(slot, block):
        if project:
            block = jnp.dot(block, weight[...], preferred_element_type=jnp.float32)
        extended[slot] = block.astype(jnp.bfloat16)

    for i in range(bound):
        put(i, halo[0, 0, i])
        put(bound + blocks + i, halo[1, 0, i])
    for i in range(blocks):
        put(bound + i, own[0, i])
    acc[...] = jnp.zeros_like(acc)

    def group(g, carry):
        products = []
        for u in range(UNROLL):
            k = g * UNROLL + u
            products.append(
                jnp.dot(vals[0, k], extended[cols[snap, k]], preferred_element_type=jnp.float32)
            )
        for u in range(UNROLL):
            row = rows[snap, g * UNROLL + u]
            acc[row] += products[u]
        return carry

    lax.fori_loop(0, vals.shape[1] // UNROLL, group, 0)
    for i in range(blocks):
        total = acc[i]
        if relu:
            total = jnp.maximum(total, 0.0)
        out[0, i] = total.astype(jnp.bfloat16)


def convolve(own, halo, tile_rows, tile_cols, tile_vals, weight, relu):
    snaps, blocks, _, width = own.shape
    bound = halo.shape[2]
    tiles = tile_vals.shape[1]
    project = weight is not None
    in_specs = [
        pl.BlockSpec((1, blocks, BS, width), lambda s, r, c: (s, 0, 0, 0)),
        pl.BlockSpec((2, 1, bound, BS, width), lambda s, r, c: (0, s, 0, 0, 0)),
        pl.BlockSpec((1, tiles, BS, BS), lambda s, r, c: (s, 0, 0, 0)),
    ]
    operands = [own, halo, tile_vals]
    if project:
        in_specs.append(pl.BlockSpec((width, width), lambda s, r, c: (0, 0)))
        operands.append(weight)
    return pl.pallas_call(
        functools.partial(conv_kernel, project, relu),
        out_shape=jax.ShapeDtypeStruct(own.shape, jnp.bfloat16),
        grid_spec=pltpu.PrefetchScalarGridSpec(
            num_scalar_prefetch=2,
            grid=(snaps,),
            in_specs=in_specs,
            out_specs=pl.BlockSpec((1, blocks, BS, width), lambda s, r, c: (s, 0, 0, 0)),
            scratch_shapes=[
                pltpu.VMEM((blocks + 2 * bound, BS, width), jnp.bfloat16),
                pltpu.VMEM((blocks, BS, width), jnp.float32),
            ],
        ),
        compiler_params=pltpu.CompilerParams(dimension_semantics=("arbitrary",)),
        cost_estimate=pl.CostEstimate(
            flops=2 * snaps * tiles * BS * BS * width, bytes_accessed=8 << 20, transcendentals=0
        ),
        name="conv_project" if project else "conv_plain",
    )(tile_rows, tile_cols, *operands)


def exchange(blocks, send_lists):
    count = lax.axis_size("vert")
    bound = send_lists.shape[1] // 2
    own_list = lax.dynamic_index_in_dim(send_lists, lax.axis_index("vert"), 0, keepdims=False)
    packed = jnp.take(blocks, own_list, axis=1)
    forward = [(i, (i + 1) % count) for i in range(count)]
    backward = [(target, source) for source, target in forward]
    low = lax.ppermute(packed[:, bound:], "vert", forward)
    high = lax.ppermute(packed[:, :bound], "vert", backward)
    return jnp.stack([low, high])


def sigmoid(x):
    return 0.5 * jnp.tanh(0.5 * x) + 0.5


def recur_kernel(
    n, conv, lstm_w, bias, proj_w, out,
    xbuf, hbuf, rbuf, h0, c0, h1, c1, send1, recv1, send2, recv2,
):
    me = lax.axis_index("snap")
    width = conv.shape[-1]
    offsets = [4, 3, 5, 2, 6, 1, 7] if n == 8 else list(range(1, n))

    barrier = pltpu.get_barrier_semaphore()
    for d in range(1, n):
        pl.semaphore_signal(
            barrier, inc=1, device_id={"snap": lax.rem(me + d, n)}, device_id_type=MESH
        )
    pl.semaphore_wait(barrier, n - 1)

    def first_copy(half, peer):
        return pltpu.make_async_remote_copy(
            src_ref=conv.at[:, 2 * peer + half],
            dst_ref=xbuf.at[half, pl.ds(2 * me, 2)],
            send_sem=send1.at[half, peer],
            recv_sem=recv1.at[half, me],
            device_id={"snap": peer},
            device_id_type=MESH,
        )

    for half in range(2):
        for d in offsets:
            first_copy(half, lax.rem(me + d, n)).start()
        pltpu.make_async_copy(
            conv.at[:, 2 * me + half], xbuf.at[half, pl.ds(2 * me, 2)], recv1.at[half, me]
        ).start()

    def cell(x, hidden, memory, layer):
        gates = (
            jnp.dot(x, lstm_w[layer, :width], preferred_element_type=jnp.float32)
            + jnp.dot(hidden[...], lstm_w[layer, width:], preferred_element_type=jnp.float32)
            + bias[layer][None, :]
        )
        kept = sigmoid(gates[:, width : 2 * width]) * memory[...]
        new = kept + sigmoid(gates[:, :width]) * jnp.tanh(gates[:, 2 * width : 3 * width])
        memory[...] = new
        result = (sigmoid(gates[:, 3 * width :]) * jnp.tanh(new)).astype(jnp.bfloat16)
        hidden[...] = result
        return result

    def second_copy(half, t, owner):
        return pltpu.make_async_remote_copy(
            src_ref=hbuf.at[half, t],
            dst_ref=rbuf.at[lax.rem(t, 2), 2 * me + half],
            send_sem=send2.at[half, t],
            recv_sem=recv2.at[half, lax.rem(t, 2), me],
            device_id={"snap": owner},
            device_id_type=MESH,
        )

    for half in range(2):
        h0[...] = jnp.zeros_like(h0)
        h1[...] = jnp.zeros_like(h1)
        c0[...] = jnp.zeros_like(c0)
        c1[...] = jnp.zeros_like(c1)

        def step(owner, carry, half=half):
            landed = xbuf.at[half, pl.ds(2 * owner, 2)]
            pltpu.make_async_copy(landed, landed, recv1.at[half, owner]).wait()
            for part in range(2):
                t = 2 * owner + part
                low = cell(xbuf[half, t], h0, c0, 0)
                hbuf[half, t] = cell(low, h1, c1, 1)

                @pl.when(owner != me)
                def _():
                    second_copy(half, t, owner).start()

                @pl.when(owner == me)
                def _():
                    pltpu.make_async_copy(
                        hbuf.at[half, t], rbuf.at[part, 2 * me + half], recv2.at[half, part, me]
                    ).start()

            return carry

        lax.fori_loop(0, n, step, 0)

    for part in range(2):
        for half in range(2):

            def finish(i, carry, half=half, part=part):
                source = lax.rem(me + i, n)
                slot = rbuf.at[part, 2 * source + half]
                pltpu.make_async_copy(slot, slot, recv2.at[half, part, source]).wait()
                out[part, 2 * source + half] = jnp.dot(
                    rbuf[part, 2 * source + half], proj_w[...], preferred_element_type=jnp.float32
                ).astype(jnp.bfloat16)
                return carry

            lax.fori_loop(0, n, finish, 0)

    for half in range(2):

        def drain(i, carry, half=half):
            peer = lax.rem(me + i, n)
            first_copy(half, peer).wait_send()
            for part in range(2):
                second_copy(half, 2 * peer + part, peer).wait_send()
            return carry

        lax.fori_loop(1, n, drain, 0)


def recur(convolved, lstm_weight, lstm_bias, proj_weight):
    n = lax.axis_size("snap")
    snaps, blocks, _, width = convolved.shape
    total = snaps * n
    vmem = pl.BlockSpec(memory_space=pltpu.VMEM)
    return pl.pallas_call(
        functools.partial(recur_kernel, n),
        out_shape=jax.ShapeDtypeStruct(convolved.shape, jnp.bfloat16),
        in_specs=[vmem] * 4,
        out_specs=vmem,
        scratch_shapes=[
            pltpu.VMEM((2, total, BS, width), jnp.bfloat16),
            pltpu.VMEM((2, total, BS, width), jnp.bfloat16),
            pltpu.VMEM((2, blocks, BS, width), jnp.bfloat16),
            pltpu.VMEM((BS, width), jnp.bfloat16),
            pltpu.VMEM((BS, width), jnp.float32),
            pltpu.VMEM((BS, width), jnp.bfloat16),
            pltpu.VMEM((BS, width), jnp.float32),
            pltpu.SemaphoreType.DMA((2, n)),
            pltpu.SemaphoreType.DMA((2, n)),
            pltpu.SemaphoreType.DMA((2, total)),
            pltpu.SemaphoreType.DMA((2, 2, n)),
        ],
        compiler_params=pltpu.CompilerParams(collective_id=0, has_side_effects=True),
        cost_estimate=pl.CostEstimate(
            flops=9 << 30, bytes_accessed=6 << 20, transcendentals=42 << 20
        ),
        name="recur",
    )(convolved, lstm_weight, lstm_bias, proj_weight)


def shards(
    features,
    tile_rows,
    tile_cols,
    tile_vals,
    send_lists,
    conv1_weight,
    conv2_weight,
    lstm_weight,
    lstm_bias,
):
    snapshots, vertices, width = features.shape
    own = features.reshape(snapshots, vertices // BS, BS, width)
    halo = exchange(own, send_lists)
    convolved = convolve(own, halo, tile_rows, tile_cols, tile_vals, conv1_weight, True)
    second = recur(convolved, lstm_weight, lstm_bias, conv2_weight)
    halo = exchange(second, send_lists)
    mixed = convolve(second, halo, tile_rows, tile_cols, tile_vals, None, False)
    return mixed.reshape(snapshots, vertices, width)


def solution(mesh):
    placed = (
        P("snap", "vert", None),
        P("snap", "vert"),
        P("snap", "vert"),
        P("snap", "vert", None, None),
        P(),
        P(),
        P(),
        P(),
        P(),
    )
    return jax.shard_map(
        shards, mesh=mesh, in_specs=placed, out_specs=P("snap", "vert", None), check_vma=False
    )
```

time: 307 us -> 151 us (0.49); the launches traced: 302 us -> 151 us
  Pallas kernels: 0 us -> 122 us
  matrix products: 72.1 us -> 0 us
  local copies, waits for them, and re-layouts: 73.4 us -> 5.35 us
  blocking collectives: 54.7 us -> 0 us
  waiting for transfers between devices: 58.4 us -> 10.9 us
  other arithmetic: 24.2 us -> 2.23 us
  starting transfers between devices: 18.4 us -> 10.3 us
    pallas_call x0 -> x3, Pallas kernels: none -> 122 us  [the longest x1 102 us: recur(): pl.pallas_call(functools.partial(recur_kernel, n), out_shape=jax.ShapeDty...]
    dot_general x38 -> x0, matrix products: 72.1 us -> none  [the longest x32 35.9 us: cell_step(): jnp.dot(jnp.concatenate([inputs, hidden], axis=-1), weight, preferred_ele...]
    all_to_all x1 -> x0, blocking collectives: 54.7 us -> none  [shards(): lax.all_to_all(recurrent, 'snap', split_axis=0, concat_axis=1, tiled=True)]
    all_to_all x1 -> x0, waiting for transfers between devices: 47.5 us -> none  [shards(): lax.all_to_all(grouped, 'snap', split_axis=1, concat_axis=0, tiled=True)]
    gather x7 -> x2, local copies, waits for them, and re-layouts: 41.3 us -> 4.38 us  [exchange(): packed = jnp.take(blocks, own_list, axis=1)]
    dot_general x2 -> x0, local copies, waits for them, and re-layouts: 24.5 us -> none  [convolve(): jnp.einsum('skij,skjf->skif', tile_vals, picked, preferred_element_type=j...]
    dynamic_update_slice x16 -> x0, other arithmetic: 15.2 us -> none  [shards(): lax.scan(advance, (zero_h, zero_c, zero_h, zero_c), sequence)]
    all_to_all x1 -> x0, starting transfers between devices: 8.1 us -> none  [shards(): lax.all_to_all(grouped, 'snap', split_axis=1, concat_axis=0, tiled=True)]
  transfers between devices with their start and end apart: 5 -> 4, of which waited for: 3 -> 2; matrix products, arithmetic and copies ran while one was open for 0% -> 0% of each run, Pallas kernels for 0% -> 0%
where the time goes in v1:
time: 151 us
  Pallas kernels  122 us (81%)
  waiting for transfers between devices  10.9 us (7%)
  starting transfers between devices  10.3 us (7%)
  local copies, waits for them, and re-layouts  5.35 us (4%)
  other arithmetic  2.23 us (1%)
    pallas_call x1, Pallas kernels, recur(): pl.pallas_call(functools.partial(recur_kernel, n), out_shape=jax.ShapeDty...  102 us
    pallas_call x2, Pallas kernels, convolve(): pl.pallas_call(functools.partial(conv_kernel, project, relu), out_shape=j...  19.4 us
    ppermute x2, waiting for transfers between devices, exchange(): low = lax.ppermute(packed[:, bound:], 'vert', forward)  10.9 us
    ppermute x2, starting transfers between devices, exchange(): high = lax.ppermute(packed[:, :bound], 'vert', backward)  10.1 us
    gather x2, local copies, waits for them, and re-layouts, exchange(): packed = jnp.take(blocks, own_list, axis=1)  4.38 us
  transfers between devices with their start and end apart: 4, of which 2 were waited for; matrix products, arithmetic and copies ran while one was open for 0% of the time, Pallas kernels for 0%

profile of v1, /device:TPU:64, one launch (start us, length us, event | category | flops | bytes accessed | tf_op | source)
XLA Modules:
  0.0 150.8 jit_solution(14523422493601009884)
XLA Ops:
  0.0 0.0 copy-start
  0.0 0.7 copy-done
  0.7 0.2 dynamic-slice_reduce_fusion
  0.9 2.2 %gather_fusion = bf16[6,2,128,256]{3,2,1,0:T(8,128)(2,1)S(1)} fusion(bf16[2,16,128,256]{3,2,1,0:T(8,128)(2,1)} %bitcast.10, s32[1024]{0:T(1024)S(1)} %pad_clamp_fusion), kind=kCustom, calls=%fused_computation.clone | custom fusion | bytes 1572888 | tf_op jit(solution)/shard_map/jit(_take)/gather | solution.py:95
  3.1 0.1 fusion.1
  3.2 0.1 fusion.3
  3.3 0.1 collective-permute-start
  3.4 5.1 %collective-permute-start.1 = (bf16[2,3,128,256]{3,2,1,0:T(8,128)(2,1)S(1)}, bf16[2,3,128,256]{3,2,1,0:T(8,128)(2,1)S(1)}, u32[]{:S(2)}, u32[]{:S(2)}) collective-permute-start(bf16[2,3,128,256]{3,2,1,0:T(8,128)(2,1)S(1)} %get-tuple-element.9), channel_id=1, source_target_pairs={{1,0},{2,1},{3,2},{4,3},{5,4},{6,5},{7,6},{8,7},{9,8},{10,9},{11,1... | collective-permute-start | bytes 1179656 | tf_op jit(solution)/shard_map/ppermute | solution.py:99
  8.5 5.5 %collective-permute-done = bf16[2,3,128,256]{3,2,1,0:T(8,128)(2,1)S(1)} collective-permute-done((bf16[2,3,128,256]{3,2,1,0:T(8,128)(2,1)S(1)}, bf16[2,3,128,256]{3,2,1,0:T(8,128)(2,1)S(1)}, u32[]{:S(2)}, u32[]{:S(2)}) %collective-permute-start) | collective-permute-done | bytes 393248 | tf_op jit(solution)/shard_map/ppermute | solution.py:98
  13.9 0.0 collective-permute-done.1
  13.9 1.0 pad_maximum_fusion.halo
  14.9 10.1 %conv_project.1.conv = bf16[2,16,128,256]{3,2,1,0:T(8,128)(2,1)} custom-call(s32[2,64]{1,0:T(2,128)} %rows.3, s32[2,64]{1,0:T(2,128)} %cols.3, bf16[2,16,128,256]{3,2,1,0:T(8,128)(2,1)} %bitcast.11, bf16[2,2,3,128,256]{4,3,2,1,0:T(8,128)(2,1)} %pad_maximum_fusion.halo, bf16[2,64,128,128]{3,2,1,0:T(8,128)(2,1)} %vals.3, bf16[256,256]{1,0:T(8,128)(2,1)} %rest_0_.1), custom_call_target="tpu_custom_call" | custom-call | flops 1073741824 | bytes 8388608 | tf_op jit(solution)/shard_map/conv_project/pallas_call | solution.py:70
  25.0 102.5 %recur.1.own = bf16[2,16,128,256]{3,2,1,0:T(8,128)(2,1)} custom-call(bf16[2,16,128,256]{3,2,1,0:T(8,128)(2,1)} %conv_project.1.conv, bf16[2,512,1024]{2,1,0:T(8,128)(2,1)} %lstm_w.1, f32[2,1024]{1,0:T(2,128)} %bias.1, bf16[256,256]{1,0:T(8,128)(2,1)} %proj_w.1), custom_call_target="tpu_custom_call" | custom-call | flops 9663676416 | bytes 6291456 | tf_op jit(solution)/shard_map/recur/pallas_call | solution.py:221
  127.5 2.2 %gather_fusion.1 = bf16[6,2,128,256]{3,2,1,0:T(8,128)(2,1)S(1)} fusion(bf16[2,16,128,256]{3,2,1,0:T(8,128)(2,1)} %recur.1.own, s32[1024]{0:T(1024)S(1)} %pad_clamp_fusion), kind=kCustom, calls=%fused_computation.1.clone | custom fusion | bytes 1572888 | tf_op jit(solution)/shard_map/jit(_take)/gather | solution.py:95
  129.7 0.1 fusion
  129.8 0.1 fusion.2
  129.9 0.1 collective-permute-start.2
  130.0 5.1 %collective-permute-start.3 = (bf16[2,3,128,256]{3,2,1,0:T(8,128)(2,1)S(1)}, bf16[2,3,128,256]{3,2,1,0:T(8,128)(2,1)S(1)}, u32[]{:S(2)}, u32[]{:S(2)}) collective-permute-start(bf16[2,3,128,256]{3,2,1,0:T(8,128)(2,1)S(1)} %get-tuple-element.7), channel_id=1, source_target_pairs={{1,0},{2,1},{3,2},{4,3},{5,4},{6,5},{7,6},{8,7},{9,8},{10,9},{11,1... | collective-permute-start | bytes 1179656 | tf_op jit(solution)/shard_map/ppermute | solution.py:99
  135.1 5.5 %collective-permute-done.2 = bf16[2,3,128,256]{3,2,1,0:T(8,128)(2,1)S(1)} collective-permute-done((bf16[2,3,128,256]{3,2,1,0:T(8,128)(2,1)S(1)}, bf16[2,3,128,256]{3,2,1,0:T(8,128)(2,1)S(1)}, u32[]{:S(2)}, u32[]{:S(2)}) %collective-permute-start.2) | collective-permute-done | bytes 393248 | tf_op jit(solution)/shard_map/ppermute | solution.py:98
  140.5 0.0 collective-permute-done.3
  140.5 1.0 pad_maximum_fusion.1.halo
  141.5 9.3 %conv_plain.1 = bf16[2,16,128,256]{3,2,1,0:T(8,128)(2,1)} custom-call(s32[2,64]{1,0:T(2,128)} %rows.3, s32[2,64]{1,0:T(2,128)} %cols.3, bf16[2,16,128,256]{3,2,1,0:T(8,128)(2,1)} %recur.1.own, bf16[2,2,3,128,256]{4,3,2,1,0:T(8,128)(2,1)} %pad_maximum_fusion.1.halo, bf16[2,64,128,128]{3,2,1,0:T(8,128)(2,1)} %vals.3), custom_call_target="tpu_custom_call" | custom-call | flops 1073741824 | bytes 8388608 | tf_op jit(solution)/shard_map/conv_plain/pallas_call | solution.py:70
  (3 shorter events, 0.0 us)
Async XLA Ops:
  0.0 0.7 copy-start
  3.3 10.6 %collective-permute-start = (bf16[2,3,128,256]{3,2,1,0:T(8,128)(2,1)S(1)}, bf16[2,3,128,256]{3,2,1,0:T(8,128)(2,1)S(1)}, u32[]{:S(2)}, u32[]{:S(2)}) collective-permute-start(bf16[2,3,128,256]{3,2,1,0:T(8,128)(2,1)S(1)} %get-tuple-element.8), channel_id=1, source_target_pairs={{0,1},{1,2},{2,3},{3,4},{4,5},{5,6},{6,7},{7,8},{8,9},{9,10},{10,1... | collective-permute-start | bytes 1179656 | tf_op jit(solution)/shard_map/ppermute | solution.py:98
  3.4 10.5 %collective-permute-start.1 = (bf16[2,3,128,256]{3,2,1,0:T(8,128)(2,1)S(1)}, bf16[2,3,128,256]{3,2,1,0:T(8,128)(2,1)S(1)}, u32[]{:S(2)}, u32[]{:S(2)}) collective-permute-start(bf16[2,3,128,256]{3,2,1,0:T(8,128)(2,1)S(1)} %get-tuple-element.9), channel_id=1, source_target_pairs={{1,0},{2,1},{3,2},{4,3},{5,4},{6,5},{7,6},{8,7},{9,8},{10,9},{11,1... | collective-permute-start | bytes 1179656 | tf_op jit(solution)/shard_map/ppermute | solution.py:99
  129.9 10.6 %collective-permute-start.2 = (bf16[2,3,128,256]{3,2,1,0:T(8,128)(2,1)S(1)}, bf16[2,3,128,256]{3,2,1,0:T(8,128)(2,1)S(1)}, u32[]{:S(2)}, u32[]{:S(2)}) collective-permute-start(bf16[2,3,128,256]{3,2,1,0:T(8,128)(2,1)S(1)} %get-tuple-element.6), channel_id=1, source_target_pairs={{0,1},{1,2},{2,3},{3,4},{4,5},{5,6},{6,7},{7,8},{8,9},{9,10},{10,1... | collective-permute-start | bytes 1179656 | tf_op jit(solution)/shard_map/ppermute | solution.py:98
  130.0 10.5 %collective-permute-start.3 = (bf16[2,3,128,256]{3,2,1,0:T(8,128)(2,1)S(1)}, bf16[2,3,128,256]{3,2,1,0:T(8,128)(2,1)S(1)}, u32[]{:S(2)}, u32[]{:S(2)}) collective-permute-start(bf16[2,3,128,256]{3,2,1,0:T(8,128)(2,1)S(1)} %get-tuple-element.7), channel_id=1, source_target_pairs={{1,0},{2,1},{3,2},{4,3},{5,4},{6,5},{7,6},{8,7},{9,8},{10,9},{11,1... | collective-permute-start | bytes 1179656 | tf_op jit(solution)/shard_map/ppermute | solution.py:99
